TPU v7x, 512 devices: a 4x2x32 block of a 4x8x32 slice. The times are simulated.
512 devices in a mesh: groups: 2 (over y), ep: 32 (over z), tp: 4 (over x), dp: 2 (over core).
Axes of the slice: x: 4, y: 2, z: 32, core: 2. Of those that a mesh axis runs over, the one named last changes fastest.
The devices are a block of a 4x8x32 slice.
Arguments:
- tokens: bfloat16 [4096, 5120], P(('groups', 'ep', 'tp', 'dp')), parts along dimension 0, may hold values from -6 to 6
- route_weights: float32 [4096, 8], P(('groups', 'ep', 'tp', 'dp')), parts along dimension 0, may hold values from 0.1 to 1
- expert_ids: int32 [4096, 8], P(('groups', 'ep', 'tp', 'dp')), parts along dimension 0, may hold values from 0 to 31, all different within a row; in each aligned block of 8 rows (0 to 7, 8 to 15, ...) at most 4 rows name the same one
- gate_weight: bfloat16 [32, 5120, 1024], P('ep', None, ('tp', 'dp')), may hold values from -0.078125 to 0.078125
- up_weight: bfloat16 [32, 5120, 1024], P('ep', None, ('tp', 'dp')), may hold values from -0.078125 to 0.078125
- down_weight: bfloat16 [32, 1024, 5120], P('ep', None, ('tp', 'dp')), may hold values from -0.1875 to 0.1875
Outputs:
- combined: bfloat16 [4096, 5120], P(('groups', 'ep', 'tp', 'dp')), parts along dimension 0
There are 2 independent parts, one for each index of `groups`. A program takes and returns all parts, laid end to end along the dimension named above; an argument that names none is the same for every part. Nothing has to cross between parts.
Inputs may be any that keep to these rules, and one draw needn't show every extreme that they name: `expert_ids`: each row names 8 different experts. Among the 8 rows of one device no expert is named more than 4 times, and in every draw some device's rows name some expert exactly 4 times.
All inputs are finite; a program needn't handle non-finite values.
Results may differ from a plain program's by a relative error of at most 0.0057.
Values may be sent and summed in bfloat16 or wider, within the bound.
A program may use at most 64 MiB of HBM per device.

v0:
```python
import jax
import jax.numpy as jnp
from jax import lax
from jax.sharding import PartitionSpec as P

CAP = 4
META = 128


def pieces(w):
    hi = w.astype(jnp.bfloat16)
    rest = w - hi.astype(jnp.float32)
    mid = rest.astype(jnp.bfloat16)
    low = (rest - mid.astype(jnp.float32)).astype(jnp.bfloat16)
    return jnp.concatenate([hi, mid, low], axis=-1)


def per_device(tokens, route_weights, expert_ids, gate_weight, up_weight, down_weight):
    n_ep = lax.axis_size("ep")
    rows, width = tokens.shape
    named = expert_ids[:, :, None] == jnp.arange(n_ep, dtype=jnp.int32)[None, None, :]
    dense = jnp.sum(jnp.where(named, route_weights[:, :, None], 0.0), axis=1)
    eye = jnp.eye(rows, dtype=jnp.bfloat16)
    meta = jnp.concatenate([pieces(dense), eye], axis=1)
    meta = jnp.pad(meta, ((0, 0), (0, META - meta.shape[1])))
    sent = jnp.concatenate([tokens, meta], axis=1)
    got = lax.all_gather(sent, "ep", axis=0)
    me = lax.axis_index("ep")

    def weight_of(block):
        m = block[..., width:].astype(jnp.float32)
        part = [lax.dynamic_slice_in_dim(m, me + j * n_ep, 1, axis=-1) for j in range(3)]
        return (part[0] + part[1] + part[2])[..., 0]

    mask = weight_of(got) > 0
    slot = jnp.cumsum(mask.astype(jnp.int32), axis=1) - 1
    pick = mask[:, None, :] & (slot[:, None, :] == jnp.arange(CAP)[None, :, None])
    sel = jnp.einsum(
        "bst,btd->bsd", pick.astype(jnp.bfloat16), got, preferred_element_type=jnp.bfloat16
    )
    piece = lax.all_gather(sel, ("tp", "dp"), axis=0)
    x = piece[..., :width]
    gate = jnp.einsum("gbsd,df->gbsf", x, gate_weight[0], preferred_element_type=jnp.float32)
    up = jnp.einsum("gbsd,df->gbsf", x, up_weight[0], preferred_element_type=jnp.float32)
    hidden = (jax.nn.silu(gate) * up).astype(jnp.bfloat16)
    hidden = lax.all_gather(hidden, ("tp", "dp"), axis=3, tiled=True)
    out = jnp.einsum(
        "gbsf,fd->gbsd", hidden, down_weight[0], preferred_element_type=jnp.float32
    ).astype(jnp.bfloat16)
    code = piece[..., width + 3 * n_ep : width + 3 * n_ep + rows]
    w = weight_of(piece)
    w_tok = jnp.sum(code.astype(jnp.float32) * w[..., None], axis=2)
    back = jnp.einsum("gbst,gbsd->bgtd", code, out, preferred_element_type=jnp.float32)
    back = (back * jnp.swapaxes(w_tok, 0, 1)[..., None]).astype(jnp.bfloat16)
    flat = back.reshape(n_ep * back.shape[1] * rows, back.shape[3])
    summed = lax.psum_scatter(flat, "ep", scatter_dimension=0, tiled=True)
    summed = summed.reshape(back.shape[1], rows, back.shape[3])
    mine = lax.all_to_all(summed, ("tp", "dp"), split_axis=0, concat_axis=2, tiled=True)
    return mine[0]


def solution(mesh):
    tok = P(("groups", "ep", "tp", "dp"), None)
    wgt = P("ep", None, ("tp", "dp"))
    return jax.shard_map(
        per_device,
        mesh=mesh,
        in_specs=(tok, tok, tok, wgt, wgt, wgt),
        out_specs=tok,
        check_vma=False,
    )
```

profile of v0, /device:TPU:33, one launch (start us, length us, event | category | flops | bytes accessed | tf_op | source)
XLA Modules:
  0.0 466.4 jit_solution(3061447939570187865)
XLA Ops:
  6.5 0.0 copy-start
  6.6 0.0 all-gather.8.cloned.1.call-start
  6.6 0.9 select_reduce_fusion
  7.5 0.1 fusion.33
  7.6 1.5 pad_maximum_fusion
  9.1 0.1 all-gather.8.cloned.1.call-update
  9.1 0.1 all-gather.10.cloned.1.call-start
  9.2 142.7 %all-gather.8.cloned.1.call-done = bf16[256,5248]{1,0:T(8,128)(2,1)} async-done(((bf16[8,5248]{1,0:T(8,128)(2,1)}), bf16[256,5248]{1,0:T(8,128)(2,1)}) %all-gather.8.cloned.1.call-update) | async-done | bytes 2686992 | tf_op jit(solution)/shard_map/all_gather | solution.py:27
  151.9 0.8 slice.16
  152.8 0.2 copy.60
  153.1 0.1 copy.49
  153.2 0.1 copy.50
  153.2 3.7 fusion.20
  156.9 0.1 all-gather.10.cloned.1.call-update
  157.0 0.0 copy-start.2
  157.0 0.1 all-gather.6.cloned.1.call-start
  157.1 88.1 %all-gather.10.cloned.1.call-done = bf16[256,4,5248]{2,1,0:T(4,128)(2,1)} async-done(((bf16[32,4,5248]{2,1,0:T(4,128)(2,1)}), bf16[256,4,5248]{2,1,0:T(4,128)(2,1)}) %all-gather.10.cloned.1.call-update) | async-done | bytes 10747920 | tf_op jit(solution)/shard_map/all_gather | solution.py:41
  245.2 7.1 %copy.51 = bf16[256,4,5248]{2,0,1:T(8,128)(2,1)S(1)} copy(bf16[256,4,5248]{2,1,0:T(4,128)(2,1)} %all-gather.10.cloned.1.call-done) | data formatting | bytes 21495808 | tf_op jit(solution)/shard_map/all_gather | solution.py:41
  252.4 0.0 copy-start.1
  252.4 0.0 copy-done.2
  252.4 0.0 copy-start.3
  252.4 2.9 fusion.2
  255.3 1.2 copy-done.1
  256.4 0.0 copy-done.3
  256.5 3.7 fusion.13
  260.2 0.1 all-gather.6.cloned.1.call-update
  260.2 0.1 reduce-scatter.2.cloned.1.call-start
  260.3 1.1 slice.17
  261.4 1.0 slice_convert_fusion
  262.4 0.5 dynamic-slice_add_fusion
  262.9 1.6 copy.59
  264.5 0.5 multiply_reduce_fusion
  265.0 39.3 %all-gather.6.cloned.1.call-done = bf16[8,32,4,1024]{3,1,2,0:T(8,128)(2,1)} async-done(((bf16[8,32,4,128]{3,1,2,0:T(8,128)(2,1)}), bf16[8,32,4,1024]{3,1,2,0:T(8,128)(2,1)}) %all-gather.6.cloned.1.call-update) | async-done | bytes 2097168 | tf_op jit(solution)/shard_map/all_gather | solution.py:46
  304.4 0.0 copy-done
  304.4 3.4 convolution_convert_fusion
  307.8 3.0 multiply_convert_fusion
  310.7 0.1 reduce-scatter.2.cloned.1.call-update
  310.8 117.5 %reduce-scatter.2.cloned.1.call-done = bf16[64,640]{1,0:T(8,128)(2,1)} async-done(((bf16[2048,640]{1,0:T(8,128)(2,1)}), bf16[64,640]{1,0:T(8,128)(2,1)}) %reduce-scatter.2.cloned.1.call-update) | async-done | bytes 81936 | tf_op jit(solution)/shard_map/reduce_scatter | solution.py:56
  428.3 30.9 %all_to_all.15 = bf16[8,8,640]{2,1,0:T(8,128)(2,1)S(1)} all-to-all(bf16[8,8,640]{2,1,0:T(8,128)(2,1)} %bitcast.51), channel_id=1, replica_groups=mesh['groups'=2,'ep'=32,'tp'=4,'dp'=2] {'tp','dp'}, dimensions={0} | all-to-all | bytes 163840 | tf_op jit(solution)/shard_map/all_to_all | solution.py:58
  459.2 0.6 copy.77
  (6 shorter events, 0.1 us)
Async XLA Ops:
  6.5 297.8 %copy-start = (bf16[1,1024,640]{2,1,0:T(8,128)(2,1)S(1)}, bf16[1,1024,640]{2,1,0:T(8,128)(2,1)}, u32[]{:S(2)}) copy-start(bf16[1,1024,640]{2,1,0:T(8,128)(2,1)} %param.11) | copy-start | bytes 3932164
  6.6 145.4 %all-gather.8.cloned.1.call-start = ((), (), s32[]{:S(2)}) async-start(), calls=%async_computation.4 | async-start | bytes 2770944 | tf_op jit(solution)/shard_map/all_gather | solution.py:27
  9.1 236.1 %all-gather.10.cloned.1.call-start = ((), (), s32[]{:S(2)}) async-start(), calls=%async_computation.5 | async-start | bytes 12091392 | tf_op jit(solution)/shard_map/all_gather | solution.py:41
  157.0 95.4 %copy-start.2 = (bf16[1,5120,128]{2,1,0:T(8,128)(2,1)S(1)}, bf16[1,5120,128]{2,1,0:T(8,128)(2,1)}, u32[]{:S(2)}) copy-start(bf16[1,5120,128]{2,1,0:T(8,128)(2,1)} %param.9) | copy-start | bytes 3932164
  157.0 147.4 %all-gather.6.cloned.1.call-start = ((), (), s32[]{:S(2)}) async-start(), calls=%async_computation.2 | async-start | bytes 2359296 | tf_op jit(solution)/shard_map/all_gather | solution.py:46
  252.4 4.1 copy-start.1
  252.4 4.1 copy-start.3
  260.2 168.0 %reduce-scatter.2.cloned.1.call-start = ((), (), s32[]{:S(2)}) async-start(), calls=%async_computation.3 | async-start | bytes 2703360 | tf_op jit(solution)/shard_map/reduce_scatter | solution.py:56
Sparse Core Ops, SparseCore 0:
  9.4 142.4 all-gather.7
  157.1 88.0 all-gather.9
  260.4 43.9 all-gather.5
  310.9 117.3 reduce-scatter.1
where the time goes:
time: 467 us; the launch traced here: 466 us
  waiting for transfers between devices  388 us (83%)
  blocking collectives  30.9 us (7%)
  matrix products  16.6 us (4%)
  between operations  13.3 us (3%)
  local copies, waits for them, and re-layouts  12.9 us (3%)
    all_gather x1, waiting for transfers between devices, per_device(): got = lax.all_gather(sent, 'ep', axis=0)  143 us
    reduce_scatter x1, waiting for transfers between devices, per_device(): summed = lax.psum_scatter(flat, 'ep', scatter_dimension=0, tiled=True)  117 us
    all_gather x1, waiting for transfers between devices, per_device(): piece = lax.all_gather(sel, ('tp', 'dp'), axis=0)  88.1 us
    all_gather x1, waiting for transfers between devices, per_device(): hidden = lax.all_gather(hidden, ('tp', 'dp'), axis=3, tiled=True)  39.3 us
    all_to_all x1, blocking collectives, per_device(): lax.all_to_all(summed, ('tp', 'dp'), split_axis=0, concat_axis=2, tiled=T...  30.9 us
  transfers between devices with their start and end apart: 4, of which 4 were waited for; matrix products, arithmetic and copies ran while one was open for 1% of the time, Pallas kernels for 0%

commit v1 on v0

--- a/solution.py
+++ b/solution.py
@@ -43,7 +43,10 @@
     gate = jnp.einsum("gbsd,df->gbsf", x, gate_weight[0], preferred_element_type=jnp.float32)
     up = jnp.einsum("gbsd,df->gbsf", x, up_weight[0], preferred_element_type=jnp.float32)
     hidden = (jax.nn.silu(gate) * up).astype(jnp.bfloat16)
-    hidden = lax.all_gather(hidden, ("tp", "dp"), axis=3, tiled=True)
+    hidden = jnp.concatenate(
+        lax.all_to_all(jnp.stack([hidden] * lax.axis_size(("tp", "dp"))), ("tp", "dp"), 0, 0),
+        axis=3,
+    )
     out = jnp.einsum(
         "gbsf,fd->gbsd", hidden, down_weight[0], preferred_element_type=jnp.float32
     ).astype(jnp.bfloat16)

time: 467 us -> 452 us (0.968)
  waiting for transfers between devices: 388 us -> 366 us
    all_gather x1 -> x0, waiting for transfers between devices: 39.3 us -> none  [per_device(): hidden = lax.all_gather(hidden, ('tp', 'dp'), axis=3, tiled=True)]
    all_to_all x0 -> x1, waiting for transfers between devices: none -> 17.4 us  [per_device(): lax.all_to_all(jnp.stack([hidden] * lax.axis_size(('tp', 'dp'))), ('tp',...]
  transfers between devices with their start and end apart: 4 -> 4, of which waited for: 4 -> 4; matrix products, arithmetic and copies ran while one was open for 1% -> 2% of each run, Pallas kernels for 0% -> 0%
where the time goes in v1:
time: 452 us
  waiting for transfers between devices  366 us (81%)
  blocking collectives  30.6 us (7%)
  local copies, waits for them, and re-layouts  16.5 us (4%)
  matrix products  14.4 us (3%)
  between operations  13.3 us (3%)
  other arithmetic  6.99 us (2%)
    all_gather x1, waiting for transfers between devices, per_device(): got = lax.all_gather(sent, 'ep', axis=0)  143 us
    reduce_scatter x1, waiting for transfers between devices, per_device(): summed = lax.psum_scatter(flat, 'ep', scatter_dimension=0, tiled=True)  117 us
    all_gather x1, waiting for transfers between devices, per_device(): piece = lax.all_gather(sel, ('tp', 'dp'), axis=0)  88.2 us
    all_to_all x1, blocking collectives, per_device(): lax.all_to_all(summed, ('tp', 'dp'), split_axis=0, concat_axis=2, tiled=T...  30.6 us
    all_to_all x1, waiting for transfers between devices, per_device(): lax.all_to_all(jnp.stack([hidden] * lax.axis_size(('tp', 'dp'))), ('tp',...  17.4 us
  transfers between devices with their start and end apart: 4, of which 4 were waited for; matrix products, arithmetic and copies ran while one was open for 2% of the time, Pallas kernels for 0%

profile of v1, /device:TPU:33, one launch (start us, length us, event | category | flops | bytes accessed | tf_op | source)
XLA Modules:
  0.0 451.6 jit_solution(490138838270041111)
XLA Ops:
  6.5 0.0 copy-start
  6.6 0.0 all-gather.5.cloned.1.call-start
  6.6 0.9 select_reduce_fusion
  7.5 0.1 fusion.39
  7.6 1.5 pad_maximum_fusion
  9.1 0.1 all-gather.5.cloned.1.call-update
  9.1 0.1 all-gather.7.cloned.1.call-start
  9.2 142.7 %all-gather.5.cloned.1.call-done = bf16[256,5248]{1,0:T(8,128)(2,1)} async-done(((bf16[8,5248]{1,0:T(8,128)(2,1)}), bf16[256,5248]{1,0:T(8,128)(2,1)}) %all-gather.5.cloned.1.call-update) | async-done | bytes 2686992 | tf_op jit(solution)/shard_map/all_gather | solution.py:27
  151.9 0.8 slice.16
  152.8 0.2 copy.66
  153.1 0.1 copy.54
  153.2 0.1 copy.55
  153.2 3.7 fusion.26
  156.9 0.1 all-gather.7.cloned.1.call-update
  157.0 0.0 copy-start.4
  157.0 88.2 %all-gather.7.cloned.1.call-done = bf16[256,4,5248]{2,1,0:T(4,128)(2,1)} async-done(((bf16[32,4,5248]{2,1,0:T(4,128)(2,1)}), bf16[256,4,5248]{2,1,0:T(4,128)(2,1)}) %all-gather.7.cloned.1.call-update) | async-done | bytes 10747920 | tf_op jit(solution)/shard_map/all_gather | solution.py:41
  245.2 7.1 %copy.56 = bf16[256,4,5248]{2,0,1:T(8,128)(2,1)S(1)} copy(bf16[256,4,5248]{2,1,0:T(4,128)(2,1)} %all-gather.7.cloned.1.call-done) | data formatting | bytes 21495808 | tf_op jit(solution)/shard_map/all_gather | solution.py:41
  252.4 0.0 copy-start.1
  252.4 0.0 copy-done.4
  252.4 0.0 copy-start.5
  252.4 2.9 fusion.2
  255.3 1.2 copy-done.1
  256.5 0.0 copy-done.5
  256.5 3.1 fusion.19
  259.5 1.8 stack.2
  261.4 3.8 all-to-all-start
  265.2 0.0 reduce-scatter.2.cloned.1.call-start
  265.2 1.8 slice.17
  267.0 1.0 slice_convert_fusion
  268.0 1.3 dynamic-slice_add_fusion
  269.2 2.6 copy.65
  271.9 2.1 multiply_reduce_fusion
  274.0 0.0 copy-start.3
  274.0 17.4 %all-to-all-done = bf16[8,8,32,4,128]{4,2,3,1,0:T(8,128)(2,1)S(1)} async-done(((bf16[8,8,32,4,128]{4,2,3,1,0:T(8,128)(2,1)}), bf16[8,8,32,4,128]{4,2,3,1,0:T(8,128)(2,1)S(1)}, u32[]{:S(2)}, u32[]{:S(2)}) %all-to-all-start) | async-done | bytes 2097184 | tf_op jit(solution)/shard_map/all_to_all | solution.py:47
  291.4 0.0 copy-done
  291.4 0.0 copy-start.2
  291.5 1.8 fusion.7
  293.2 0.0 copy-done.3
  293.3 0.0 copy-done.2
  293.3 3.0 multiply_convert_fusion
  296.2 0.1 reduce-scatter.2.cloned.1.call-update
  296.3 117.5 %reduce-scatter.2.cloned.1.call-done = bf16[64,640]{1,0:T(8,128)(2,1)} async-done(((bf16[2048,640]{1,0:T(8,128)(2,1)}), bf16[64,640]{1,0:T(8,128)(2,1)}) %reduce-scatter.2.cloned.1.call-update) | async-done | bytes 81936 | tf_op jit(solution)/shard_map/reduce_scatter | solution.py:59
  413.8 30.6 %all_to_all.20 = bf16[8,8,640]{2,1,0:T(8,128)(2,1)S(1)} all-to-all(bf16[8,8,640]{2,1,0:T(8,128)(2,1)} %bitcast.60), channel_id=1, replica_groups=mesh['groups'=2,'ep'=32,'tp'=4,'dp'=2] {'tp','dp'}, dimensions={0} | all-to-all | bytes 163840 | tf_op jit(solution)/shard_map/all_to_all | solution.py:61
  444.4 0.6 copy.90
  (6 shorter events, 0.1 us)
Async XLA Ops:
  6.5 284.9 %copy-start = (bf16[1,1024,640]{2,1,0:T(8,128)(2,1)S(1)}, bf16[1,1024,640]{2,1,0:T(8,128)(2,1)}, u32[]{:S(2)}) copy-start(bf16[1,1024,640]{2,1,0:T(8,128)(2,1)} %param.11) | copy-start | bytes 3932164
  6.6 145.4 %all-gather.5.cloned.1.call-start = ((), (), s32[]{:S(2)}) async-start(), calls=%async_computation.4 | async-start | bytes 2770944 | tf_op jit(solution)/shard_map/all_gather | solution.py:27
  9.1 236.1 %all-gather.7.cloned.1.call-start = ((), (), s32[]{:S(2)}) async-start(), calls=%async_computation.5 | async-start | bytes 12091392 | tf_op jit(solution)/shard_map/all_gather | solution.py:41
  157.0 95.4 %copy-start.4 = (bf16[1,5120,128]{2,1,0:T(8,128)(2,1)S(1)}, bf16[1,5120,128]{2,1,0:T(8,128)(2,1)}, u32[]{:S(2)}) copy-start(bf16[1,5120,128]{2,1,0:T(8,128)(2,1)} %param.9) | copy-start | bytes 3932164
  252.4 4.1 copy-start.1
  252.4 4.1 copy-start.5
  261.4 30.1 %all-to-all-start = ((bf16[8,8,32,4,128]{4,2,3,1,0:T(8,128)(2,1)}), bf16[8,8,32,4,128]{4,2,3,1,0:T(8,128)(2,1)S(1)}, u32[]{:S(2)}, u32[]{:S(2)}) async-start(bf16[8,8,32,4,128]{4,2,3,1,0:T(8,128)(2,1)} %stack.2), calls=%async_computation | async-start | bytes 4194304 | tf_op jit(solution)/shard_map/all_to_all | solution.py:47
  265.2 148.6 %reduce-scatter.2.cloned.1.call-start = ((), (), s32[]{:S(2)}) async-start(), calls=%async_computation.3 | async-start | bytes 2703360 | tf_op jit(solution)/shard_map/reduce_scatter | solution.py:59
  274.0 19.3 %copy-start.3 = (f32[8,32,8]{2,0,1:T(8,128)S(1)}, f32[8,32,8]{2,0,1:T(8,128)}, u32[]{:S(2)}) copy-start(f32[8,32,8]{2,0,1:T(8,128)} %multiply_reduce_fusion) | copy-start | bytes 24580
  291.4 1.8 copy-start.2
Sparse Core Ops, SparseCore 0:
  9.4 142.4 all-gather.4
  157.1 88.0 all-gather.6
  296.4 117.3 reduce-scatter.1
